TPU v7x, 32 devices: a whole 2x2x4 slice. The times are simulated.
32 devices in a mesh: dp: 16 (over z, x, core), ens: 2 (over y).
Axes of the slice: x: 2, y: 2, z: 4, core: 2. Of those that a mesh axis runs over, the one named last changes fastest.
Arguments:
- embeddings: bfloat16 [12288, 1024], P('dp'), may hold values from -6 to 6
- valid_mask: int32 [12288], P('dp'), may hold values 0 or 1
- first_weight: bfloat16 [2, 1024, 4096], P(None, 'dp', 'ens'), may hold values from -0.1875 to 0.1875
- second_weight: bfloat16 [2, 4096, 128], P(None, 'ens'), may hold values from -0.09375 to 0.09375
- thresholds: int32 [2], replicated, may hold values from -256 to 256
Outputs:
- mean_logits: float32 [12288, 128], P('dp')
- kept_share: float32 [2], P('ens')
- agree_share: float32 [2], P('ens')
All inputs are finite; a program needn't handle non-finite values. No bound on the sum of `valid_mask` on one device may be relied on, other than what follows from the above.
Results may differ from a plain program's by a relative error of at most 0.0044.
Values may be sent and summed in bfloat16 or wider, within the bound.
A program may use at most 64 MiB of HBM per device.

v0:
```python
import jax
import jax.numpy as jnp
from jax import lax
from jax.sharding import PartitionSpec as P


def on_device(embeddings, valid_mask, first_weight, second_weight, thresholds):
    member = lax.axis_index("ens")
    own_first = lax.all_to_all(first_weight, "ens", split_axis=0, concat_axis=2, tiled=True)
    own_second = lax.all_to_all(second_weight, "ens", split_axis=0, concat_axis=1, tiled=True)
    full_first = lax.all_gather(own_first[0], "dp", axis=0, tiled=True)
    hidden = jnp.maximum(
        jnp.dot(embeddings, full_first, preferred_element_type=jnp.float32), 0.0
    ).astype(jnp.bfloat16)
    logits_own = jnp.dot(hidden, own_second[0], preferred_element_type=jnp.float32)
    classes = logits_own.shape[1]
    levels = jnp.arange(classes, dtype=jnp.float32)
    grades = (2.0 * levels / (classes - 1) - 1.0) * jnp.sqrt(jnp.float32(3.0 / classes))
    scores = jnp.dot(logits_own, grades, precision=lax.Precision.HIGHEST)
    cutoffs = thresholds.astype(jnp.float32) / 256.0
    own_cutoff = lax.dynamic_index_in_dim(cutoffs, member, 0, keepdims=False)
    validity = valid_mask.astype(jnp.float32)
    kept_soft = validity * jax.nn.sigmoid(4.0 * (scores - own_cutoff))
    kept_total = lax.psum(jnp.sum(kept_soft), "dp")
    mean_logits = lax.psum(logits_own, "ens") / first_weight.shape[0]
    ens_score = jnp.dot(mean_logits, grades, precision=lax.Precision.HIGHEST)
    ens_kept = jax.nn.sigmoid(4.0 * (ens_score - jnp.mean(cutoffs)))
    agree_local = jnp.sum(kept_soft * ens_kept)
    agree_total = lax.psum(agree_local, "dp")
    shard_docs = embeddings.shape[0]
    return (
        mean_logits,
        (kept_total / shard_docs).reshape(1),
        (agree_total / shard_docs).reshape(1),
    )


def solution(mesh):
    return jax.shard_map(
        on_device,
        mesh=mesh,
        in_specs=(P("dp", None), P("dp"), P(None, "dp", "ens"), P(None, "ens", None), P()),
        out_specs=(P("dp", None), P("ens"), P("ens")),
        check_vma=False,
    )
```

profile of v0, /device:TPU:0, one launch (start us, length us, event | category | flops | bytes accessed | tf_op | source)
XLA Modules:
  0.0 184.1 jit_solution(3838105246013471597)
XLA Ops:
  7.2 0.0 copy-start
  7.2 0.0 all-gather.2.cloned.1.call-start
  7.2 13.1 %all_to_all.24 = bf16[2,64,2048]{2,1,0:T(8,128)(2,1)S(1)} all-to-all(bf16[2,64,2048]{2,1,0:T(8,128)(2,1)} %param.7), channel_id=1, replica_groups=mesh['dp'=16,'ens'=2] {'ens'}, dimensions={0} | all-to-all | bytes 1048576 | tf_op jit(solution)/shard_map/all_to_all | solution.py:9
  20.4 0.5 copy.8
  20.9 1.0 copy.9
  21.9 0.0 all-gather.2.cloned.1.call-update
  21.9 16.9 %all_to_all.25 = bf16[2,2048,128]{2,1,0:T(8,128)(2,1)S(1)} all-to-all(bf16[2,2048,128]{2,1,0:T(8,128)(2,1)} %param.8), channel_id=1, replica_groups=mesh['dp'=16,'ens'=2] {'ens'}, dimensions={0} | all-to-all | bytes 2097152 | tf_op jit(solution)/shard_map/all_to_all | solution.py:10
  38.8 58.1 %all-gather.2.cloned.1.call-done = bf16[1024,4096]{1,0:T(8,128)(2,1)} async-done(((bf16[64,4096]{1,0:T(8,128)(2,1)}), bf16[1024,4096]{1,0:T(8,128)(2,1)}) %all-gather.2.cloned.1.call-update) | async-done | bytes 8388624 | tf_op jit(solution)/shard_map/all_gather | solution.py:11
  96.9 0.0 copy-done
  96.9 0.0 copy-start.4
  96.9 0.0 copy-start.3
  96.9 11.8 %fusion = f32[768,128]{1,0:T(8,128)S(1)} fusion(bf16[4096,128]{1,0:T(8,128)(2,1)S(1)} %bitcast.24, bf16[768,1024]{1,0:T(8,128)(2,1)S(1)} %copy-done, bf16[1024,4096]{1,0:T(8,128)(2,1)} %all-gather.2.cloned.1.call-done), kind=kOutput, calls=%fused_computation.1 | convolution fusion | flops 7254048768 | bytes 11403264 | tf_op jit(solution)/shard_map/dot_general | solution.py:15
  108.7 0.0 copy-start.1
  108.7 0.5 convolution_reduce_fusion.1
  109.2 0.0 all-reduce.3.cloned.1.call-start
  109.2 0.2 copy-done.1
  109.5 0.5 all-reduce.3.cloned.1.call-update
  109.9 0.0 copy-done.4
  110.0 0.6 convert_multiply_fusion
  111.2 0.6 dynamic_slice.4
  111.8 25.5 %all-reduce.3.cloned.1.call-done = f32[768,128]{1,0:T(8,128)} async-done(((f32[768,128]{1,0:T(8,128)}), f32[768,128]{1,0:T(8,128)}) %all-reduce.3.cloned.1.call-update) | async-done | bytes 393232 | tf_op jit(solution)/shard_map/psum | solution.py:25
  137.3 1.0 broadcast_multiply_fusion
  138.3 0.0 copy-start.2
  138.3 0.5 convolution_reduce_fusion
  138.8 0.0 copy-done.3
  138.8 1.3 multiply_reduce_fusion
  140.1 33.6 %all-reduce = (f32[]{:T(128)}, f32[]{:T(128)}) all-reduce(f32[]{:T(128)} %get-tuple-element.4, f32[]{:T(128)} %get-tuple-element.3), channel_id=1, replica_groups=mesh['dp'=16,'ens'=2] {'dp'}, use_global_device_ids=true, to_apply=%region_2.3 | all-reduce | flops 2 | bytes 16 | tf_op jit(solution)/shard_map/psum | solution.py:24
  175.0 0.0 copy-done.2
Async XLA Ops:
  7.2 89.7 %copy-start = (bf16[768,1024]{1,0:T(8,128)(2,1)S(1)}, bf16[768,1024]{1,0:T(8,128)(2,1)}, u32[]{:S(2)}) copy-start(bf16[768,1024]{1,0:T(8,128)(2,1)} %param.5) | copy-start | bytes 4718596
  7.2 89.7 %all-gather.2.cloned.1.call-start = ((), (), s32[]{:S(2)}) async-start(), calls=%async_computation.2 | async-start | bytes 8912896 | tf_op jit(solution)/shard_map/all_gather | solution.py:11
  96.9 13.1 %copy-start.4 = (s32[2]{0:T(128)S(1)}, s32[2]{0:T(128)}, u32[]{:S(2)}) copy-start(s32[2]{0:T(128)} %param.9) | copy-start | bytes 28
  96.9 41.9 %copy-start.3 = (s32[768]{0:T(1024)S(1)}, s32[768]{0:T(1024)}, u32[]{:S(2)}) copy-start(s32[768]{0:T(1024)} %param.6) | copy-start | bytes 9220
  108.7 0.8 copy-start.1
  109.2 28.1 %all-reduce.3.cloned.1.call-start = ((), (), s32[]{:S(2)}) async-start(), calls=%async_computation.3 | async-start | bytes 786432 | tf_op jit(solution)/shard_map/psum | solution.py:25
  138.3 36.7 %copy-start.2 = (f32[768,128]{1,0:T(8,128)}, f32[768,128]{1,0:T(8,128)S(1)}, u32[]{:S(2)}) copy-start(f32[768,128]{1,0:T(8,128)S(1)} %broadcast_multiply_fusion) | copy-start | bytes 1179652
Sparse Core Ops, SparseCore 0:
  22.1 74.7 all-gather.1
  112.9 24.3 all-reduce.2
where the time goes:
time: 184 us
  waiting for transfers between devices  84 us (46%)
  blocking collectives  63.6 us (35%)
  between operations  18.2 us (10%)
  matrix products  12.7 us (7%)
  other arithmetic  2.97 us (2%)
  local copies, waits for them, and re-layouts  2.4 us (1%)
    all_gather x1, waiting for transfers between devices, on_device(): full_first = lax.all_gather(own_first[0], 'dp', axis=0, tiled=True)  58.1 us
    psum x1, blocking collectives, on_device(): kept_total = lax.psum(jnp.sum(kept_soft), 'dp')  33.6 us
    psum x1, waiting for transfers between devices, on_device(): mean_logits = lax.psum(logits_own, 'ens') / first_weight.shape[0]  25.5 us
    all_to_all x1, blocking collectives, on_device(): lax.all_to_all(second_weight, 'ens', split_axis=0, concat_axis=1, tiled=T...  16.9 us
    all_to_all x1, blocking collectives, on_device(): lax.all_to_all(first_weight, 'ens', split_axis=0, concat_axis=2, tiled=True)  13.1 us
    dot_general x1, matrix products, on_device(): jnp.dot(hidden, own_second[0], preferred_element_type=jnp.float32)  11.8 us
  transfers between devices with their start and end apart: 2, of which 2 were waited for; matrix products, arithmetic and copies ran while one was open for 1% of the time, Pallas kernels for 0%

commit v1 on v0

v1 whole, which is shorter than its diff:
```python
import jax
import jax.numpy as jnp
from jax import lax
from jax.sharding import PartitionSpec as P


def on_device(embeddings, valid_mask, first_weight, second_weight, thresholds):
    members, rows, units = first_weight.shape
    member = lax.axis_index("ens")
    own = members // lax.axis_size("ens")
    full_first = lax.all_gather(first_weight, "dp", axis=1, tiled=True)
    partial = []
    for m in range(members):
        hidden = jnp.maximum(
            jnp.dot(embeddings, full_first[m], preferred_element_type=jnp.float32), 0.0
        ).astype(jnp.bfloat16)
        partial.append(jnp.dot(hidden, second_weight[m], preferred_element_type=jnp.float32))
    classes = partial[0].shape[1]
    levels = jnp.arange(classes, dtype=jnp.float32)
    grades = (2.0 * levels / (classes - 1) - 1.0) * jnp.sqrt(jnp.float32(3.0 / classes))
    scores = jnp.stack([jnp.dot(p, grades, precision=lax.Precision.HIGHEST) for p in partial])
    mean_logits, scores = lax.psum((sum(partial) / members, scores), "ens")
    cutoffs = thresholds.astype(jnp.float32) / 256.0
    own_scores = lax.dynamic_slice_in_dim(scores, member * own, own, 0)
    own_cutoffs = lax.dynamic_slice_in_dim(cutoffs, member * own, own, 0)
    validity = valid_mask.astype(jnp.float32)
    kept = validity * jax.nn.sigmoid(4.0 * (own_scores - own_cutoffs[:, None]))
    ens_kept = jax.nn.sigmoid(4.0 * (jnp.mean(scores, axis=0) - jnp.mean(cutoffs)))
    sums = jnp.stack([jnp.sum(kept, axis=1), jnp.sum(kept * ens_kept, axis=1)])
    sums = lax.psum(sums, "dp") / embeddings.shape[0]
    return mean_logits, sums[0], sums[1]


def solution(mesh):
    return jax.shard_map(
        on_device,
        mesh=mesh,
        in_specs=(P("dp", None), P("dp"), P(None, "dp", "ens"), P(None, "ens", None), P()),
        out_specs=(P("dp", None), P("ens"), P("ens")),
        check_vma=False,
    )
```

time: 184 us -> 149 us (0.81)
  blocking collectives: 63.6 us -> 35.1 us
  waiting for transfers between devices: 84 us -> 76.8 us
  between operations: 18.2 us -> 14.7 us
  matrix products: 12.7 us -> 14.7 us
    all_to_all x2 -> x0, blocking collectives: 30 us -> none  [the longest x1 16.9 us: on_device(): lax.all_to_all(second_weight, 'ens', split_axis=0, concat_axis=1, tiled=T...]
    psum x1, waiting for transfers between devices: 25.5 us -> 0.01 us  [on_device(): mean_logits, scores = lax.psum((sum(partial) / members, scores), 'ens')]
    all_gather x1, waiting for transfers between devices: 58.1 us -> 76.1 us  [on_device(): full_first = lax.all_gather(first_weight, 'dp', axis=1, tiled=True)]
    dot_general x3 -> x4, matrix products: 12.7 us -> 14.7 us  [the longest x2 13.9 us: on_device(): jnp.dot(hidden, second_weight[m], preferred_element_type=jnp.float32)]
    psum x1 -> x2, blocking collectives: 33.6 us -> 35.1 us  [the longest x1 30.1 us: on_device(): sums = lax.psum(sums, 'dp') / embeddings.shape[0]]
  transfers between devices with their start and end apart: 2 -> 2, of which waited for: 2 -> 1; matrix products, arithmetic and copies ran while one was open for 1% -> 4% of each run, Pallas kernels for 0% -> 0%
where the time goes in v1:
time: 149 us
  waiting for transfers between devices  76.8 us (52%)
  blocking collectives  35.1 us (24%)
  matrix products  14.7 us (10%)
  between operations  14.7 us (10%)
  other arithmetic  4.66 us (3%)
  local copies, waits for them, and re-layouts  2.9 us (2%)
    all_gather x1, waiting for transfers between devices, on_device(): full_first = lax.all_gather(first_weight, 'dp', axis=1, tiled=True)  76.1 us
    psum x1, blocking collectives, on_device(): sums = lax.psum(sums, 'dp') / embeddings.shape[0]  30.1 us
    dot_general x2, matrix products, on_device(): jnp.dot(hidden, second_weight[m], preferred_element_type=jnp.float32)  13.9 us
    psum x1, blocking collectives, on_device(): mean_logits, scores = lax.psum((sum(partial) / members, scores), 'ens')  4.99 us
  transfers between devices with their start and end apart: 2, of which 1 were waited for; matrix products, arithmetic and copies ran while one was open for 4% of the time, Pallas kernels for 0%

profile of v1, /device:TPU:0, one launch (start us, length us, event | category | flops | bytes accessed | tf_op | source)
XLA Modules:
  0.0 149.0 jit_solution(6562644324986032395)
XLA Ops:
  7.2 0.0 copy-start
  7.2 0.0 all-gather.2.cloned.1.call-start
  7.2 0.7 all-gather.2.cloned.1.call-update
  7.9 0.0 all-reduce.2.cloned.1.call-start
  8.0 0.7 convert_element_type.14
  8.7 1.3 fusion.21
  10.6 0.6 dynamic_slice.7
  11.2 0.0 copy-start.1
  11.2 76.1 %all-gather.2.cloned.1.call-done = bf16[2,1024,2048]{2,1,0:T(8,128)(2,1)} async-done(((bf16[2,64,2048]{2,1,0:T(8,128)(2,1)}), bf16[2,1024,2048]{2,1,0:T(8,128)(2,1)}) %all-gather.2.cloned.1.call-update) | async-done | bytes 8388624 | tf_op jit(solution)/shard_map/all_gather | solution.py:11
  87.3 0.0 copy-done
  87.3 6.6 %fusion.3 = f32[768,128]{1,0:T(8,128)S(1)} fusion(bf16[768,1024]{1,0:T(8,128)(2,1)S(1)} %copy-done, bf16[2,1024,2048]{2,1,0:T(8,128)(2,1)} %all-gather.2.cloned.1.call-done, bf16[2,2048,128]{2,1,0:T(8,128)(2,1)} %param.8), kind=kOutput, calls=%fused_computation.7 | convolution fusion | flops 3627024384 | bytes 6684672 | tf_op jit(solution)/shard_map/dot_general | solution.py:17
  93.9 0.4 fusion.9
  94.3 0.0 copy-done.1
  94.3 7.3 %add_multiply_fusion = (f32[768,128]{1,0:T(8,128)}, f32[768,128]{1,0:T(8,128)S(1)}) fusion(f32[768,128]{1,0:T(8,128)S(1)} %fusion.3, bf16[2,2048,128]{2,1,0:T(8,128)(2,1)S(1)} %copy-done.1, bf16[768,1024]{1,0:T(8,128)(2,1)S(1)} %copy-done, bf16[2,1024,2048]{2,1,0:T(8,128)(2,1)} %all-gather.2.cloned.1.call-done), kind=kOutput, calls=%fused_computation.12 | convolution fusion | flops 3627220992 | bytes 7471104 | tf_op jit(solution)/shard_map/dot_general | solution.py:17
  101.6 0.4 fusion.11
  102.0 0.1 pad_maximum_fusion
  102.1 5.0 %psum.22 = f32[2,768]{1,0:T(2,128)S(1)} all-reduce(f32[2,768]{1,0:T(2,128)S(1)} %pad_maximum_fusion), channel_id=1, replica_groups=mesh['dp'=16,'ens'=2] {'ens'}, use_global_device_ids=true, to_apply=%region_1.0 | all-reduce | flops 1536 | bytes 12288 | tf_op jit(solution)/shard_map/psum | solution.py:22
  107.1 0.0 all-reduce.2.cloned.1.call-update
  107.2 1.3 fusion.22
  108.5 1.3 pad_maximum_fusion.1
  109.8 30.1 %psum.23 = f32[2,1]{1,0:T(2,128)S(1)} all-reduce(f32[2,1]{1,0:T(2,128)S(1)} %pad_maximum_fusion.1), channel_id=1, replica_groups=mesh['dp'=16,'ens'=2] {'dp'}, use_global_device_ids=true, to_apply=%region_6.0 | all-reduce | flops 2 | bytes 16 | tf_op jit(solution)/shard_map/psum | solution.py:30
  139.9 0.5 fusion.23
  140.4 0.0 all-reduce.2.cloned.1.call-done
  140.4 1.8 %copy.9 = f32[768,128]{1,0:T(8,128)} copy(f32[768,128]{1,0:T(8,128)} %all-reduce.2.cloned.1.call-done) | data formatting | bytes 786432
  (3 shorter events, 0.0 us)
Async XLA Ops:
  7.2 80.1 %copy-start = (bf16[768,1024]{1,0:T(8,128)(2,1)S(1)}, bf16[768,1024]{1,0:T(8,128)(2,1)}, u32[]{:S(2)}) copy-start(bf16[768,1024]{1,0:T(8,128)(2,1)} %param.5) | copy-start | bytes 4718596
  7.2 80.1 %all-gather.2.cloned.1.call-start = ((), (), s32[]{:S(2)}) async-start(), calls=%async_computation | async-start | bytes 8912896 | tf_op jit(solution)/shard_map/all_gather | solution.py:11
  7.9 132.5 %all-reduce.2.cloned.1.call-start = ((), (), s32[]{:S(2)}) async-start(), calls=%async_computation.1 | async-start | bytes 786432 | tf_op jit(solution)/shard_map/psum | solution.py:22
  11.2 83.2 %copy-start.1 = (bf16[2,2048,128]{2,1,0:T(8,128)(2,1)S(1)}, bf16[2,2048,128]{2,1,0:T(8,128)(2,1)}, u32[]{:S(2)}) copy-start(bf16[2,2048,128]{2,1,0:T(8,128)(2,1)} %param.8) | copy-start | bytes 3145732
Sparse Core Ops, SparseCore 0:
  10.2 77.0 all-gather.1
  107.2 24.3 all-reduce.1

commit v2 on v1

v2 whole, which is shorter than its diff:
```python
import functools

import jax
import jax.numpy as jnp
from jax import lax
from jax.experimental import pallas as pl
from jax.experimental.pallas import tpu as pltpu
from jax.sharding import PartitionSpec as P

MESH = pl.DeviceIdType.MESH
COLS = 256
LAG = 1
PARTS = 2


def geometry(mesh):
    line = [tuple(d.coords) for d in mesh.devices.reshape(mesh.devices.shape[0], -1)[:, 0]]
    cores = sum(c == line[0] for c in line)
    chips = line[::cores]
    inner = 1
    if len(chips) > 1:
        axis = [a != b for a, b in zip(chips[0], chips[1])].index(True)
        while inner < len(chips) and chips[inner][axis] == chips[0][axis] + inner:
            inner += 1
    return len(chips) // inner, inner, cores


def turned_period(nz, nx):
    even = (nz - 1) * nx - (nx - 1)
    slope = (nz - 1) * (nx - 1) + (nz - 1) * (nx - 1)
    share = 1.0 - even / slope if slope else 0.0
    return round(1 / share) if share > 0 else 0


def kernel(
    geo, n_ens, emb_hbm, mask_ref, fw_hbm, sw_hbm, thr_ref, out_ref, kept_ref, agree_ref,
    w, emb, sw, acc, part, sc, tot,
    local_sem, emb_sem, send_sem, recv_sem, part_send, part_recv, sc_send, sc_recv, tot_send, tot_recv,
):
    nz, nx, nc = geo
    n_dp = nz * nx * nc
    n_chips = nz * nx
    members, rows, units = fw_hbm.shape
    per_member = units // COLS
    chunks = members * per_member
    docs, classes = out_ref.shape
    period = turned_period(nz, nx)
    reach = nz - 1 + nx - 1
    slots = send_sem.shape[0]

    me = lax.axis_index("dp")
    ens = lax.axis_index("ens")
    core = lax.rem(me, nc)
    chip = me // nc
    z, x = chip // nx, lax.rem(chip, nx)

    def origin_rows(origin):
        return pl.ds(pl.multiple_of(origin * rows, rows), rows)

    def own_copy(c):
        cols = pl.ds(pl.multiple_of(lax.rem(c, per_member) * COLS, COLS), COLS)
        return pltpu.make_async_copy(
            fw_hbm.at[c // per_member, :, cols], w.at[c, origin_rows(me), :], local_sem.at[c]
        )

    for c in range(chunks):
        own_copy(jnp.int32(c)).start()
    emb_copy = pltpu.make_async_copy(emb_hbm, emb, emb_sem.at[0])
    sw_copy = pltpu.make_async_copy(sw_hbm, sw, emb_sem.at[1])
    emb_copy.start()
    sw_copy.start()

    barrier = pltpu.get_barrier_semaphore()
    dirs = []
    if nz > 1:
        dirs += [("z", 1), ("z", -1)]
    if nx > 1:
        dirs += [("x", 1), ("x", -1)]
    dirs += [("c", k) for k in range(1, nc)]

    def target(d):
        kind, k = d
        if kind == "z":
            return me + k * nx * nc
        if kind == "x":
            return me + k * nc
        return chip * nc + lax.rem(core + k, nc)

    def there(d):
        kind, k = d
        if kind == "c":
            return None
        at, n = (z, nz) if kind == "z" else (x, nx)
        return at + 1 < n if k > 0 else at > 0

    waits = jnp.int32(nc - 1 + n_ens - 1)
    for d in dirs:
        ok = there(d)
        if ok is None:
            pl.semaphore_signal(barrier, inc=1, device_id={"dp": target(d)}, device_id_type=MESH)
        else:
            @pl.when(ok)
            def _():
                pl.semaphore_signal(barrier, inc=1, device_id={"dp": target(d)}, device_id_type=MESH)
            waits = waits + ok.astype(jnp.int32)
    for k in range(1, n_ens):
        pl.semaphore_signal(
            barrier, inc=1, device_id={"ens": lax.rem(ens + k, n_ens)}, device_id_type=MESH
        )
    pl.semaphore_wait(barrier, waits)

    def turned(c):
        if not period:
            return jnp.bool_(False)
        return lax.rem(c, period) == period // 2

    def goes(d, c, zo, xo):
        kind, k = d
        if kind == "c":
            return c >= 0
        inner_first = turned(c)
        if kind == "z":
            away = (z >= zo) if k > 0 else (z <= zo)
            return away & there(d) & ((xo == x) | inner_first)
        away = (x >= xo) if k > 0 else (x <= xo)
        return away & there(d) & ((zo == z) | jnp.logical_not(inner_first))

    def sending(i, d, c, zo, xo):
        place = zo * nx + xo
        origin = place * nc + core
        block = w.at[c, origin_rows(origin), :]
        return pltpu.make_async_remote_copy(
            src_ref=block, dst_ref=block,
            send_sem=send_sem.at[lax.rem(c, slots), i, place], recv_sem=recv_sem.at[c, origin],
            device_id={"dp": target(d)}, device_id_type=MESH,
        )

    def arrived(c, origin):
        block = w.at[c, origin_rows(origin), :]
        pltpu.make_async_remote_copy(
            src_ref=block, dst_ref=block, send_sem=send_sem.at[0, 0, 0], recv_sem=recv_sem.at[c, origin],
            device_id={"dp": target(dirs[-1])}, device_id_type=MESH,
        ).wait_recv()

    def place_of(k):
        kz, kx = divmod(k, nx)
        return lax.rem(z + kz, nz), lax.rem(x + kx, nx)

    acc[...] = jnp.zeros_like(acc)

    def step(t, carry):
        for k in range(n_chips):
            zo, xo = place_of(k)
            c = t - LAG * (jnp.abs(z - zo) + jnp.abs(x - xo))

            @pl.when((c >= 0) & (c < chunks))
            def _():
                if k == 0:
                    own_copy(c).wait()
                else:
                    arrived(c, (zo * nx + xo) * nc + core)
                for i, d in enumerate(dirs):
                    @pl.when((c >= slots) & goes(d, c - slots, zo, xo))
                    def _():
                        sending(i, d, c - slots, zo, xo).wait_send()

                    @pl.when(goes(d, c, zo, xo))
                    def _():
                        sending(i, d, c, zo, xo).start()

        done = t - LAG * reach - 1

        @pl.when(done >= 0)
        def _():
            @pl.when(done == 0)
            def _():
                emb_copy.wait()
                sw_copy.wait()
            for k in range(n_chips):
                for o in range(1, nc):
                    arrived(done, k * nc + lax.rem(core + o, nc))
            m = done // per_member
            cols = pl.ds(pl.multiple_of(lax.rem(done, per_member) * COLS, COLS), COLS)
            hidden = jnp.maximum(
                jnp.dot(emb[...], w[done], preferred_element_type=jnp.float32), 0.0
            ).astype(jnp.bfloat16)
            acc[m] += jnp.dot(hidden, sw[m, cols, :], preferred_element_type=jnp.float32)
        return carry

    lax.fori_loop(0, chunks + LAG * reach + 1, step, 0)

    lines = sc.shape[1]
    levels = lax.broadcasted_iota(jnp.int32, (lines, classes), 1).astype(jnp.float32)
    grades = (2.0 * levels / (classes - 1) - 1.0) * jnp.sqrt(jnp.float32(3.0 / classes))
    line = lax.broadcasted_iota(jnp.int32, (lines, classes), 0)
    own_scores = jnp.zeros((lines, docs), jnp.float32)
    for m in range(members):
        own_scores += lax.dot_general(
            jnp.where(line == m, grades, 0.0), acc[m], (((1,), (1,)), ((), ())),
            precision=lax.Precision.HIGHEST, preferred_element_type=jnp.float32,
        )
    sc[ens] = own_scores

    def sc_copy(k):
        return pltpu.make_async_remote_copy(
            src_ref=sc.at[ens], dst_ref=sc.at[ens], send_sem=sc_send.at[k], recv_sem=sc_recv.at[ens],
            device_id={"ens": lax.rem(ens + k, n_ens)}, device_id_type=MESH,
        )

    def part_copy(k, b):
        piece = part.at[ens, pl.ds(b * (docs // PARTS), docs // PARTS), :]
        return pltpu.make_async_remote_copy(
            src_ref=piece, dst_ref=piece, send_sem=part_send.at[k, b], recv_sem=part_recv.at[ens, b],
            device_id={"ens": lax.rem(ens + k, n_ens)}, device_id_type=MESH,
        )

    for k in range(1, n_ens):
        sc_copy(k).start()
    for b in range(PARTS):
        piece = pl.ds(b * (docs // PARTS), docs // PARTS)
        total = acc[0, piece, :]
        for m in range(1, members):
            total += acc[m, piece, :]
        part[ens, piece, :] = (total * (1.0 / members)).astype(jnp.bfloat16)
        for k in range(1, n_ens):
            part_copy(k, b).start()

    for k in range(1, n_ens):
        other = lax.rem(ens + k, n_ens)
        pltpu.make_async_remote_copy(
            src_ref=sc.at[other], dst_ref=sc.at[other], send_sem=sc_send.at[k], recv_sem=sc_recv.at[other],
            device_id={"ens": other}, device_id_type=MESH,
        ).wait_recv()
    scores = sc[0]
    for k in range(1, n_ens):
        scores += sc[k]
    row = lax.broadcasted_iota(jnp.int32, (lines, docs), 0)
    cutoff = jnp.zeros((lines, docs), jnp.float32)
    mean_cutoff = jnp.float32(0.0)
    for m in range(members):
        level = thr_ref[m].astype(jnp.float32) * (1.0 / 256.0)
        cutoff = jnp.where(row == m, level, cutoff)
        mean_cutoff += level * (1.0 / members)
    kept = mask_ref[...].astype(jnp.float32) * jax.nn.sigmoid(4.0 * (scores - cutoff))
    ens_score = jnp.sum(scores, axis=0, keepdims=True) * (1.0 / members)
    ens_kept = jax.nn.sigmoid(4.0 * (ens_score - mean_cutoff))
    kept_sum = jnp.sum(kept, axis=1, keepdims=True)
    agree_sum = jnp.sum(kept * ens_kept, axis=1, keepdims=True)
    lane = lax.broadcasted_iota(jnp.int32, (lines, 128), 1)
    tot[me] = jnp.where(lane == 0, kept_sum, jnp.where(lane == 1, agree_sum, 0.0))

    def tot_copy(k):
        return pltpu.make_async_remote_copy(
            src_ref=tot.at[me], dst_ref=tot.at[me], send_sem=tot_send.at[k], recv_sem=tot_recv.at[me],
            device_id={"dp": lax.rem(me + k, n_dp)}, device_id_type=MESH,
        )

    for k in range(1, n_dp):
        tot_copy(k).start()

    for b in range(PARTS):
        piece = pl.ds(b * (docs // PARTS), docs // PARTS)
        for k in range(1, n_ens):
            other = lax.rem(ens + k, n_ens)
            block = part.at[other, piece, :]
            pltpu.make_async_remote_copy(
                src_ref=block, dst_ref=block, send_sem=part_send.at[k, b], recv_sem=part_recv.at[other, b],
                device_id={"ens": other}, device_id_type=MESH,
            ).wait_recv()
        total = part[0, piece, :].astype(jnp.float32)
        for k in range(1, n_ens):
            total += part[k, piece, :].astype(jnp.float32)
        out_ref[piece, :] = total

    for k in range(1, n_dp):
        other = lax.rem(me + k, n_dp)
        pltpu.make_async_remote_copy(
            src_ref=tot.at[other], dst_ref=tot.at[other], send_sem=tot_send.at[k], recv_sem=tot_recv.at[other],
            device_id={"dp": other}, device_id_type=MESH,
        ).wait_recv()
    sums = tot[0]
    for k in range(1, n_dp):
        sums += tot[k]
    sums = sums / docs
    own = members // n_ens
    row = lax.broadcasted_iota(jnp.int32, (lines, 128), 0)
    for j in range(own):
        mine = row == ens * own + j
        kept_ref[j] = jnp.sum(jnp.where(mine & (lane == 0), sums, 0.0))
        agree_ref[j] = jnp.sum(jnp.where(mine & (lane == 1), sums, 0.0))

    for k in range(n_chips):
        zo, xo = place_of(k)
        for c in range(max(0, chunks - slots), chunks):
            for i, d in enumerate(dirs):
                @pl.when(goes(d, jnp.int32(c), zo, xo))
                def _():
                    sending(i, d, jnp.int32(c), zo, xo).wait_send()
    for k in range(1, n_ens):
        sc_copy(k).wait_send()
        for b in range(PARTS):
            part_copy(k, b).wait_send()
    for k in range(1, n_dp):
        tot_copy(k).wait_send()


def solution(mesh):
    geo = geometry(mesh)
    nz, nx, nc = geo
    n_dp, n_ens = mesh.shape["dp"], mesh.shape["ens"]

    def on_device(embeddings, valid_mask, first_weight, second_weight, thresholds):
        docs, width = embeddings.shape
        members, rows, units = first_weight.shape
        classes = second_weight.shape[2]
        chunks = members * units // COLS
        own = members // n_ens
        lines = -(-members // 8) * 8
        dma = pltpu.SemaphoreType.DMA
        hbm, vmem, smem = (pl.BlockSpec(memory_space=s) for s in (pl.ANY, pltpu.VMEM, pltpu.SMEM))
        return pl.pallas_call(
            functools.partial(kernel, geo, n_ens),
            out_shape=(
                jax.ShapeDtypeStruct((docs, classes), jnp.float32),
                jax.ShapeDtypeStruct((own,), jnp.float32),
                jax.ShapeDtypeStruct((own,), jnp.float32),
            ),
            in_specs=[hbm, vmem, hbm, hbm, smem],
            out_specs=(vmem, smem, smem),
            scratch_shapes=[
                pltpu.VMEM((chunks, width, COLS), jnp.bfloat16),
                pltpu.VMEM((docs, width), jnp.bfloat16),
                pltpu.VMEM(second_weight.shape, jnp.bfloat16),
                pltpu.VMEM((members, docs, classes), jnp.float32),
                pltpu.VMEM((n_ens, docs, classes), jnp.bfloat16),
                pltpu.VMEM((n_ens, lines, docs), jnp.float32),
                pltpu.VMEM((n_dp, lines, 128), jnp.float32),
                dma((chunks,)),
                dma((2,)),
                dma((2, 4 + nc - 1, nz * nx)),
                dma((chunks, n_dp)),
                dma((n_ens, PARTS)),
                dma((n_ens, PARTS)),
                dma((n_ens,)),
                dma((n_ens,)),
                dma((n_dp,)),
                dma((n_dp,)),
            ],
            compiler_params=pltpu.CompilerParams(
                collective_id=0, has_side_effects=True, vmem_limit_bytes=48 * 1024 * 1024
            ),
        )(embeddings, valid_mask.reshape(1, docs), first_weight, second_weight, thresholds)

    return jax.shard_map(
        on_device,
        mesh=mesh,
        in_specs=(P("dp", None), P("dp"), P(None, "dp", "ens"), P(None, "ens", None), P()),
        out_specs=(P("dp", None), P("ens"), P("ens")),
        check_vma=False,
    )
```

time: 149 us -> 85.2 us (0.57)
  waiting for transfers between devices: 76.8 us -> 0 us
  Pallas kernels: 0 us -> 75.1 us
  blocking collectives: 35.1 us -> 0 us
  matrix products: 14.7 us -> 0 us
  between operations: 14.7 us -> 4.08 us
  other arithmetic: 4.66 us -> 0 us
  local copies, waits for them, and re-layouts: 2.9 us -> 5.77 us
    all_gather x1 -> x0, waiting for transfers between devices: 76.1 us -> none  [on_device(): full_first = lax.all_gather(first_weight, 'dp', axis=1, tiled=True)]
    pallas_call x0 -> x1, Pallas kernels: none -> 75.1 us  [on_device(): pl.pallas_call(functools.partial(kernel, geo, n_ens), out_shape=(jax.Shap...]
    psum x2 -> x0, blocking collectives: 35.1 us -> none  [the longest x1 30.1 us: on_device(): sums = lax.psum(sums, 'dp') / embeddings.shape[0]]
    dot_general x4 -> x0, matrix products: 14.7 us -> none  [the longest x2 13.9 us: on_device(): jnp.dot(hidden, second_weight[m], preferred_element_type=jnp.float32)]
    unnamed x5 -> x9, local copies, waits for them, and re-layouts: 1.79 us -> 5.08 us
    reduce_sum x3 -> x0, other arithmetic: 2.62 us -> none  [the longest x1 1.34 us: on_device(): sums = jnp.stack([jnp.sum(kept, axis=1), jnp.sum(kept * ens_kept, axis=1)])]
  transfers between devices with their start and end apart: 2 -> 0, of which waited for: 1 -> 0; matrix products, arithmetic and copies ran while one was open for 4% -> 0% of each run, Pallas kernels for 0% -> 0%
where the time goes in v2:
time: 85.2 us; the launch traced here: 84.9 us
  Pallas kernels  75.1 us (88%)
  local copies, waits for them, and re-layouts  5.77 us (7%)
  between operations  4.08 us (5%)
    pallas_call x1, Pallas kernels, on_device(): pl.pallas_call(functools.partial(kernel, geo, n_ens), out_shape=(jax.Shap...  75.1 us
    unnamed x9, local copies, waits for them, and re-layouts  5.08 us

profile of v2, /device:TPU:0, one launch (start us, length us, event | category | flops | bytes accessed | tf_op | source)
XLA Modules:
  0.0 84.9 jit_solution(4123519892634250015)
XLA Ops:
  0.6 0.7 reshape.9.mask_ref
  1.3 0.0 copy-start
  1.3 1.4 %copy-done = bf16[768,1024]{1,0:T(8,128)(2,1)S(1)} copy-done((bf16[768,1024]{1,0:T(8,128)(2,1)S(1)}, bf16[768,1024]{1,0:T(8,128)(2,1)}, u32[]{:S(2)}) %copy-start) | copy-done | bytes 1572888
  2.7 0.0 copy-start.1
  2.7 1.2 %copy-done.1 = bf16[2,2048,128]{2,1,0:T(8,128)(2,1)S(1)} copy-done((bf16[2,2048,128]{2,1,0:T(8,128)(2,1)S(1)}, bf16[2,2048,128]{2,1,0:T(8,128)(2,1)}, u32[]{:S(2)}) %copy-start.1) | copy-done | bytes 1048600
  4.0 0.0 copy-start.2
  4.0 1.0 %copy-done.2 = bf16[2,64,2048]{2,1,0:T(8,128)(2,1)S(1)} copy-done((bf16[2,64,2048]{2,1,0:T(8,128)(2,1)S(1)}, bf16[2,64,2048]{2,1,0:T(8,128)(2,1)}, u32[]{:S(2)}) %copy-start.2) | copy-done | bytes 524312
  5.0 0.0 copy-start.3
  5.0 0.7 copy-done.3
  5.7 75.1 %shard_map.76 = (f32[768,128]{1,0:T(8,128)S(1)}, f32[1]{0:T(128)}, f32[1]{0:T(128)}) custom-call(bf16[768,1024]{1,0:T(8,128)(2,1)S(1)} %copy-done, s32[1,768]{1,0:T(1,128)S(1)} %reshape.9.mask_ref, bf16[2,64,2048]{2,1,0:T(8,128)(2,1)S(1)} %copy-done.2, bf16[2,2048,128]{2,1,0:T(8,128)(2,1)S(1)} %copy-done.1, s32[2]{0:T(128)S(1)} %copy-done.3), custom_call_target="tpu_custom_call" | custom-call | tf_op jit(solution)/shard_map/pallas_call | solution.py:321
  80.7 0.7 copy.11
Async XLA Ops:
  1.3 1.4 %copy-start = (bf16[768,1024]{1,0:T(8,128)(2,1)S(1)}, bf16[768,1024]{1,0:T(8,128)(2,1)}, u32[]{:S(2)}) copy-start(bf16[768,1024]{1,0:T(8,128)(2,1)} %emb_hbm.1) | copy-start | bytes 4718596
  2.7 1.2 %copy-start.1 = (bf16[2,2048,128]{2,1,0:T(8,128)(2,1)S(1)}, bf16[2,2048,128]{2,1,0:T(8,128)(2,1)}, u32[]{:S(2)}) copy-start(bf16[2,2048,128]{2,1,0:T(8,128)(2,1)} %sw_hbm.1) | copy-start | bytes 3145732
  4.0 1.0 %copy-start.2 = (bf16[2,64,2048]{2,1,0:T(8,128)(2,1)S(1)}, bf16[2,64,2048]{2,1,0:T(8,128)(2,1)}, u32[]{:S(2)}) copy-start(bf16[2,64,2048]{2,1,0:T(8,128)(2,1)} %fw_hbm.1) | copy-start | bytes 1572868
  5.0 0.7 copy-start.3

commit v3 on v2

--- a/solution.py
+++ b/solution.py
@@ -8,9 +8,10 @@
 from jax.sharding import PartitionSpec as P
 
 MESH = pl.DeviceIdType.MESH
-COLS = 256
-LAG = 1
+COLS = 512
+LAG = 2
 PARTS = 2
+SLOTS = 2
 
 
 def geometry(mesh):
@@ -112,7 +113,7 @@
     def turned(c):
         if not period:
             return jnp.bool_(False)
-        return lax.rem(c, period) == period // 2
+        return lax.rem(c * nc + core, period) == period // 2
 
     def goes(d, c, zo, xo):
         kind, k = d
@@ -148,28 +149,7 @@
 
     acc[...] = jnp.zeros_like(acc)
 
-    def step(t, carry):
-        for k in range(n_chips):
-            zo, xo = place_of(k)
-            c = t - LAG * (jnp.abs(z - zo) + jnp.abs(x - xo))
-
-            @pl.when((c >= 0) & (c < chunks))
-            def _():
-                if k == 0:
-                    own_copy(c).wait()
-                else:
-                    arrived(c, (zo * nx + xo) * nc + core)
-                for i, d in enumerate(dirs):
-                    @pl.when((c >= slots) & goes(d, c - slots, zo, xo))
-                    def _():
-                        sending(i, d, c - slots, zo, xo).wait_send()
-
-                    @pl.when(goes(d, c, zo, xo))
-                    def _():
-                        sending(i, d, c, zo, xo).start()
-
-        done = t - LAG * reach - 1
-
+    def compute(done):
         @pl.when(done >= 0)
         def _():
             @pl.when(done == 0)
@@ -185,6 +165,29 @@
                 jnp.dot(emb[...], w[done], preferred_element_type=jnp.float32), 0.0
             ).astype(jnp.bfloat16)
             acc[m] += jnp.dot(hidden, sw[m, cols, :], preferred_element_type=jnp.float32)
+
+    def step(t, carry):
+        for k in range(n_chips):
+            zo, xo = place_of(k)
+            c = t - LAG * (jnp.abs(z - zo) + jnp.abs(x - xo))
+
+            @pl.when((c >= 0) & (c < chunks))
+            def _():
+                if k == 0:
+                    own_copy(c).wait()
+                else:
+                    arrived(c, (zo * nx + xo) * nc + core)
+                for i, d in enumerate(dirs):
+                    @pl.when((c >= slots) & goes(d, c - slots, zo, xo))
+                    def _():
+                        sending(i, d, c - slots, zo, xo).wait_send()
+
+                    @pl.when(goes(d, c, zo, xo))
+                    def _():
+                        sending(i, d, c, zo, xo).start()
+
+            if k == n_chips - 1:
+                compute(t - LAG * reach - 1)
         return carry
 
     lax.fori_loop(0, chunks + LAG * reach + 1, step, 0)
@@ -241,7 +244,7 @@
         level = thr_ref[m].astype(jnp.float32) * (1.0 / 256.0)
         cutoff = jnp.where(row == m, level, cutoff)
         mean_cutoff += level * (1.0 / members)
-    kept = mask_ref[...].astype(jnp.float32) * jax.nn.sigmoid(4.0 * (scores - cutoff))
+    kept = mask_ref[...].reshape(1, docs).astype(jnp.float32) * jax.nn.sigmoid(4.0 * (scores - cutoff))
     ens_score = jnp.sum(scores, axis=0, keepdims=True) * (1.0 / members)
     ens_kept = jax.nn.sigmoid(4.0 * (ens_score - mean_cutoff))
     kept_sum = jnp.sum(kept, axis=1, keepdims=True)
@@ -337,7 +340,7 @@
                 pltpu.VMEM((n_dp, lines, 128), jnp.float32),
                 dma((chunks,)),
                 dma((2,)),
-                dma((2, 4 + nc - 1, nz * nx)),
+                dma((SLOTS, 4 + nc - 1, nz * nx)),
                 dma((chunks, n_dp)),
                 dma((n_ens, PARTS)),
                 dma((n_ens, PARTS)),
@@ -347,9 +350,9 @@
                 dma((n_dp,)),
             ],
             compiler_params=pltpu.CompilerParams(
-                collective_id=0, has_side_effects=True, vmem_limit_bytes=48 * 1024 * 1024
+                collective_id=0, has_side_effects=True, vmem_limit_bytes=63 * 1024 * 1024
             ),
-        )(embeddings, valid_mask.reshape(1, docs), first_weight, second_weight, thresholds)
+        )(embeddings, valid_mask, first_weight, second_weight, thresholds)
 
     return jax.shard_map(
         on_device,

time: 85.2 us -> 70.6 us (0.83)
  Pallas kernels: 75.1 us -> 64.4 us
  local copies, waits for them, and re-layouts: 5.77 us -> 1.77 us
    pallas_call x1, Pallas kernels: 75.1 us -> 64.4 us  [on_device(): pl.pallas_call(functools.partial(kernel, geo, n_ens), out_shape=(jax.Shap...]
    unnamed x9 -> x1, local copies, waits for them, and re-layouts: 5.08 us -> 1.77 us
where the time goes in v3:
time: 70.6 us; the launch traced here: 70.4 us
  Pallas kernels  64.4 us (91%)
  between operations  4.21 us (6%)
  local copies, waits for them, and re-layouts  1.77 us (3%)
    pallas_call x1, Pallas kernels, on_device(): pl.pallas_call(functools.partial(kernel, geo, n_ens), out_shape=(jax.Shap...  64.4 us
    unnamed x1, local copies, waits for them, and re-layouts  1.77 us

profile of v3, /device:TPU:0, one launch (start us, length us, event | category | flops | bytes accessed | tf_op | source)
XLA Modules:
  0.0 70.4 jit_solution(7563605359740860117)
XLA Ops:
  0.6 64.4 %shard_map.76 = (f32[768,128]{1,0:T(8,128)}, f32[1]{0:T(128)}, f32[1]{0:T(128)}) custom-call(bf16[768,1024]{1,0:T(8,128)(2,1)} %emb_hbm.1, s32[768]{0:T(1024)} %mask_ref.1, bf16[2,64,2048]{2,1,0:T(8,128)(2,1)} %fw_hbm.1, bf16[2,2048,128]{2,1,0:T(8,128)(2,1)} %sw_hbm.1, s32[2]{0:T(128)} %thr_ref.1), custom_call_target="tpu_custom_call" | custom-call | tf_op jit(solution)/shard_map/pallas_call | solution.py:324
  65.1 1.8 %copy.11 = f32[768,128]{1,0:T(8,128)} copy(f32[768,128]{1,0:T(8,128)} %get-tuple-element.6) | data formatting | bytes 786432

commit v4 on v3

--- a/solution.py
+++ b/solution.py
@@ -36,7 +36,7 @@
 def kernel(
     geo, n_ens, emb_hbm, mask_ref, fw_hbm, sw_hbm, thr_ref, out_ref, kept_ref, agree_ref,
     w, emb, sw, acc, part, sc, tot,
-    local_sem, emb_sem, send_sem, recv_sem, part_send, part_recv, sc_send, sc_recv, tot_send, tot_recv,
+    local_sem, emb_sem, send_sem, recv_sem, part_send, part_recv, sc_send, sc_recv, tot_sem, core_send, core_recv,
 ):
     nz, nx, nc = geo
     n_dp = nz * nx * nc
@@ -130,16 +130,27 @@
         place = zo * nx + xo
         origin = place * nc + core
         block = w.at[c, origin_rows(origin), :]
-        return pltpu.make_async_remote_copy(
-            src_ref=block, dst_ref=block,
-            send_sem=send_sem.at[lax.rem(c, slots), i, place], recv_sem=recv_sem.at[c, origin],
+        if d[0] == "c":
+            sems = core_send.at[c, d[1]], core_recv.at[c, d[1]]
+        else:
+            sems = send_sem.at[lax.rem(c, slots), i, place], recv_sem.at[c, place]
+        return pltpu.make_async_remote_copy(
+            src_ref=block, dst_ref=block, send_sem=sems[0], recv_sem=sems[1],
             device_id={"dp": target(d)}, device_id_type=MESH,
         )
 
-    def arrived(c, origin):
-        block = w.at[c, origin_rows(origin), :]
+    def from_cores(c, k):
+        blocks = w.at[c, pl.ds(0, n_chips * rows), :]
+        return pltpu.make_async_remote_copy(
+            src_ref=blocks, dst_ref=blocks,
+            send_sem=core_send.at[c, k], recv_sem=core_recv.at[c, k],
+            device_id={"dp": target(("c", k))}, device_id_type=MESH,
+        )
+
+    def arrived(c, place):
+        block = w.at[c, origin_rows(place * nc + core), :]
         pltpu.make_async_remote_copy(
-            src_ref=block, dst_ref=block, send_sem=send_sem.at[0, 0, 0], recv_sem=recv_sem.at[c, origin],
+            src_ref=block, dst_ref=block, send_sem=send_sem.at[0, 0, 0], recv_sem=recv_sem.at[c, place],
             device_id={"dp": target(dirs[-1])}, device_id_type=MESH,
         ).wait_recv()
 
@@ -156,9 +167,8 @@
             def _():
                 emb_copy.wait()
                 sw_copy.wait()
-            for k in range(n_chips):
-                for o in range(1, nc):
-                    arrived(done, k * nc + lax.rem(core + o, nc))
+            for o in range(1, nc):
+                from_cores(done, o).wait_recv()
             m = done // per_member
             cols = pl.ds(pl.multiple_of(lax.rem(done, per_member) * COLS, COLS), COLS)
             hidden = jnp.maximum(
@@ -176,8 +186,12 @@
                 if k == 0:
                     own_copy(c).wait()
                 else:
-                    arrived(c, (zo * nx + xo) * nc + core)
+                    arrived(c, zo * nx + xo)
                 for i, d in enumerate(dirs):
+                    if d[0] == "c":
+                        sending(i, d, c, zo, xo).start()
+                        continue
+
                     @pl.when((c >= slots) & goes(d, c - slots, zo, xo))
                     def _():
                         sending(i, d, c - slots, zo, xo).wait_send()
@@ -254,9 +268,15 @@
 
     def tot_copy(k):
         return pltpu.make_async_remote_copy(
-            src_ref=tot.at[me], dst_ref=tot.at[me], send_sem=tot_send.at[k], recv_sem=tot_recv.at[me],
+            src_ref=tot.at[me], dst_ref=tot.at[me], send_sem=tot_sem.at[0], recv_sem=tot_sem.at[1],
             device_id={"dp": lax.rem(me + k, n_dp)}, device_id_type=MESH,
         )
+
+    tiles = tot.at[pl.ds(0, n_dp - 1)]
+    all_tot = pltpu.make_async_remote_copy(
+        src_ref=tiles, dst_ref=tiles, send_sem=tot_sem.at[0], recv_sem=tot_sem.at[1],
+        device_id={"dp": lax.rem(me + 1, n_dp)}, device_id_type=MESH,
+    )
 
     for k in range(1, n_dp):
         tot_copy(k).start()
@@ -275,12 +295,7 @@
             total += part[k, piece, :].astype(jnp.float32)
         out_ref[piece, :] = total
 
-    for k in range(1, n_dp):
-        other = lax.rem(me + k, n_dp)
-        pltpu.make_async_remote_copy(
-            src_ref=tot.at[other], dst_ref=tot.at[other], send_sem=tot_send.at[k], recv_sem=tot_recv.at[other],
-            device_id={"dp": other}, device_id_type=MESH,
-        ).wait_recv()
+    all_tot.wait_recv()
     sums = tot[0]
     for k in range(1, n_dp):
         sums += tot[k]
@@ -296,15 +311,18 @@
         zo, xo = place_of(k)
         for c in range(max(0, chunks - slots), chunks):
             for i, d in enumerate(dirs):
-                @pl.when(goes(d, jnp.int32(c), zo, xo))
-                def _():
-                    sending(i, d, jnp.int32(c), zo, xo).wait_send()
+                if d[0] != "c":
+                    @pl.when(goes(d, jnp.int32(c), zo, xo))
+                    def _():
+                        sending(i, d, jnp.int32(c), zo, xo).wait_send()
+    for c in range(chunks):
+        for k in range(1, nc):
+            from_cores(c, k).wait_send()
     for k in range(1, n_ens):
         sc_copy(k).wait_send()
         for b in range(PARTS):
             part_copy(k, b).wait_send()
-    for k in range(1, n_dp):
-        tot_copy(k).wait_send()
+    all_tot.wait_send()
 
 
 def solution(mesh):
@@ -340,14 +358,15 @@
                 pltpu.VMEM((n_dp, lines, 128), jnp.float32),
                 dma((chunks,)),
                 dma((2,)),
-                dma((SLOTS, 4 + nc - 1, nz * nx)),
-                dma((chunks, n_dp)),
+                dma((SLOTS, 4, nz * nx)),
+                dma((chunks, nz * nx)),
                 dma((n_ens, PARTS)),
                 dma((n_ens, PARTS)),
                 dma((n_ens,)),
                 dma((n_ens,)),
-                dma((n_dp,)),
-                dma((n_dp,)),
+                dma((2,)),
+                dma((chunks, nc)),
+                dma((chunks, nc)),
             ],
             compiler_params=pltpu.CompilerParams(
                 collective_id=0, has_side_effects=True, vmem_limit_bytes=63 * 1024 * 1024

time: 70.6 us -> 69.8 us (0.989)
  Pallas kernels: 64.4 us -> 63.6 us
    pallas_call x1, Pallas kernels: 64.4 us -> 63.6 us  [on_device(): pl.pallas_call(functools.partial(kernel, geo, n_ens), out_shape=(jax.Shap...]
where the time goes in v4:
time: 69.8 us; the launch traced here: 69.6 us
  Pallas kernels  63.6 us (91%)
  between operations  4.21 us (6%)
  local copies, waits for them, and re-layouts  1.77 us (3%)
    pallas_call x1, Pallas kernels, on_device(): pl.pallas_call(functools.partial(kernel, geo, n_ens), out_shape=(jax.Shap...  63.6 us
    unnamed x1, local copies, waits for them, and re-layouts  1.77 us

profile of v4, /device:TPU:0, one launch (start us, length us, event | category | flops | bytes accessed | tf_op | source)
XLA Modules:
  0.0 69.6 jit_solution(7199199657719422946)
XLA Ops:
  0.6 63.6 %shard_map.76 = (f32[768,128]{1,0:T(8,128)}, f32[1]{0:T(128)}, f32[1]{0:T(128)}) custom-call(bf16[768,1024]{1,0:T(8,128)(2,1)} %emb_hbm.1, s32[768]{0:T(1024)} %mask_ref.1, bf16[2,64,2048]{2,1,0:T(8,128)(2,1)} %fw_hbm.1, bf16[2,2048,128]{2,1,0:T(8,128)(2,1)} %sw_hbm.1, s32[2]{0:T(128)} %thr_ref.1), custom_call_target="tpu_custom_call" | custom-call | tf_op jit(solution)/shard_map/pallas_call | solution.py:342
  64.3 1.8 %copy.11 = f32[768,128]{1,0:T(8,128)} copy(f32[768,128]{1,0:T(8,128)} %get-tuple-element.6) | data formatting | bytes 786432
